TPU v7x, 32 devices: a whole 2x2x4 slice. The times are simulated.
32 devices in a mesh: src: 4 (over y, core), dst: 8 (over z, x).
Axes of the slice: x: 2, y: 2, z: 4, core: 2. Of those that a mesh axis runs over, the one named last changes fastest.
Arguments:
- features: bfloat16 [8192, 768], P(('src', 'dst')), may hold values from -6 to 6
- edge_tiles: bfloat16 [4, 8, 64, 128, 128], P('src', 'dst'), may hold values from -0.3125 to 0.3125
- tile_src: int32 [4, 8, 64], P('src', 'dst'), may hold values from 0 to 7
- tile_dst: int32 [4, 8, 64], P('src', 'dst'), may hold values from 0 to 15, as said below
- tile_count: int32 [4, 8], P('src', 'dst'), may hold values from 1 to 64, as said below
- weight: bfloat16 [768, 1024], replicated, may hold values from -0.21875 to 0.21875
- out_bias: float32 [1024], replicated, may hold values from -3 to 3
- out_grad: bfloat16 [8192, 1024], P(('src', 'dst')), may hold values from -6 to 6
Outputs:
- hidden: bfloat16 [8192, 1024], P(('src', 'dst'))
- feature_grad: bfloat16 [8192, 768], P(('src', 'dst'))
- weight_grad: float32 [768, 1024], replicated
- bias_grad: float32 [1024], replicated
Inputs may be any that keep to these rules, and one draw needn't show every extreme that they name: `tile_src`: block s of the source column of device (i, k) is block s % 2 of device (s // 2, k). `tile_dst`: block e of the destination row of device (i, k) is block e % 2 of device (i, e // 2). On one device, all tile slots whose destination blocks lie on one device name the same block. In every row of devices, slot 0 of every device names one common block. `tile_count`: some device uses all 64 slots.
All inputs are finite; a program needn't handle non-finite values.
Results may differ from a plain program's by a relative error of at most 0.024.
Values may be sent and summed in bfloat16 or wider, within the bound.
A program may use at most 128 MiB of HBM per device.

v0:
```python
import jax
import jax.numpy as jnp
from jax import lax
from jax.experimental import pallas as pl
from jax.experimental.pallas import tpu as pltpu
from jax.sharding import PartitionSpec as P


def block_matrix_kernel(blocks, src_ref, dst_ref, count_ref, tiles_ref, out_ref, total):
    size = tiles_ref.shape[1]
    total[...] = jnp.zeros_like(total)

    def add_tile(slot, carry):
        row = pl.multiple_of(dst_ref[slot] // blocks * size, size)
        col = pl.multiple_of(src_ref[slot] * size, size)
        total[pl.ds(row, size), pl.ds(col, size)] += tiles_ref[slot].astype(jnp.float32)
        return carry

    lax.fori_loop(0, count_ref[0], add_tile, 0)
    out_ref[...] = total[...].astype(out_ref.dtype)


def block_matrix(src_ids, dst_ids, tile_total, tiles, blocks, masters, columns):
    size = tiles.shape[1]
    shape = (masters * size, columns * size)
    smem = pl.BlockSpec(memory_space=pltpu.SMEM)
    vmem = pl.BlockSpec(memory_space=pltpu.VMEM)
    held = tiles.size * 2 + shape[0] * shape[1] * 6
    return pl.pallas_call(
        lambda *refs: block_matrix_kernel(blocks, *refs),
        out_shape=jax.ShapeDtypeStruct(shape, jnp.bfloat16),
        in_specs=[smem, smem, smem, vmem],
        out_specs=vmem,
        scratch_shapes=[pltpu.VMEM(shape, jnp.float32)],
        compiler_params=pltpu.CompilerParams(vmem_limit_bytes=held + 4 * 1024 * 1024),
        cost_estimate=pl.CostEstimate(flops=tiles.size, bytes_accessed=held, transcendentals=0),
        name="block_matrix",
    )(src_ids, dst_ids, tile_total, tiles)


def scatter_sum(terms):
    chips = terms.shape[0]
    holders = chips * 2
    me = lax.axis_index("src")
    core = me % 2
    chip = me // 2
    kept = jnp.where(core == 0, terms[:, 0], terms[:, 1])
    given = jnp.where(core == 0, terms[:, 1], terms[:, 0]).astype(jnp.bfloat16)
    got = lax.ppermute(given, "src", [(i, i ^ 1) for i in range(holders)])
    pair = kept + got.astype(jnp.float32)
    result = lax.dynamic_index_in_dim(pair, chip, 0, keepdims=False)
    sent = pair.astype(jnp.bfloat16)
    for step in range(1, chips):
        out = lax.dynamic_index_in_dim(sent, (chip + step) % chips, 0, keepdims=False)
        ring = [(i, (i + 2 * step) % holders) for i in range(holders)]
        result = result + lax.ppermute(out, "src", ring).astype(jnp.float32)
    return result.astype(jnp.bfloat16)


def per_device(features, edge_tiles, tile_src, tile_dst, tile_count, weight, out_bias, out_grad):
    capacity = edge_tiles.shape[2]
    edge_size = edge_tiles.shape[3]
    feat_width = features.shape[1]
    block_rows = features.shape[0]
    blocks = block_rows // edge_size
    masters = lax.axis_size("dst")
    holders = lax.axis_size("src")
    adjacency = edge_tiles.reshape(capacity, edge_size, edge_size)
    src_ids = tile_src.reshape(capacity)
    dst_ids = tile_dst.reshape(capacity)
    tile_total = tile_count.reshape(())
    alive_mask = jnp.arange(capacity, dtype=jnp.int32) < tile_total
    block_ids = jnp.arange(blocks, dtype=jnp.int32)
    owner_ids = dst_ids // blocks
    inner_ids = dst_ids % blocks
    column = lax.all_gather(features, "src", axis=0, tiled=True)
    matrix = block_matrix(
        src_ids, dst_ids, tile_count.reshape(1), adjacency, blocks, masters, holders * blocks
    )
    routing = (owner_ids[None, :] == jnp.arange(masters, dtype=jnp.int32)[:, None]) & alive_mask[
        None, :
    ]
    wanted_block = jnp.max(jnp.where(routing, inner_ids[None, :], 0), axis=1)
    wanted_rows = jnp.broadcast_to(wanted_block[:, None], (masters, edge_size))
    asked = lax.all_to_all(wanted_rows, "dst", split_axis=0, concat_axis=0, tiled=True)
    outgoing = jnp.dot(matrix, column, preferred_element_type=jnp.float32).astype(jnp.bfloat16)
    incoming = lax.all_to_all(
        outgoing.reshape(masters, edge_size, feat_width),
        "dst",
        split_axis=0,
        concat_axis=0,
        tiled=True,
    )
    asked_block = asked[:, 0]
    selector = asked_block[:, None] == block_ids[None, :]
    aggregate = jnp.concatenate(
        [
            jnp.sum(
                jnp.where(selector[:, j, None, None], incoming.astype(jnp.float32), 0.0), axis=0
            ).astype(jnp.bfloat16)
            for j in range(blocks)
        ],
        axis=0,
    )
    preact = jnp.dot(aggregate, weight, preferred_element_type=jnp.float32) + out_bias
    gate_value = jax.nn.sigmoid(preact)
    hidden = (preact * gate_value).astype(jnp.bfloat16)
    pre_grad = out_grad.astype(jnp.float32) * (gate_value * (1.0 + preact * (1.0 - gate_value)))
    pre_grad_b = pre_grad.astype(jnp.bfloat16)
    weight_term = lax.dot_general(
        aggregate, pre_grad_b, (((0,), (0,)), ((), ())), preferred_element_type=jnp.float32
    )
    bias_term = jnp.sum(pre_grad, axis=0, keepdims=True)
    joined = jnp.concatenate(
        [weight_term.astype(jnp.bfloat16), jnp.broadcast_to(bias_term, (16, bias_term.shape[1])).astype(jnp.bfloat16)],
        axis=0,
    )
    reduced = lax.psum(joined, ("src", "dst"))
    weight_grad = reduced[:feat_width].astype(jnp.float32)
    bias_grad = reduced[feat_width].astype(jnp.float32)
    back = lax.dot_general(
        pre_grad_b, weight, (((1,), (1,)), ((), ())), preferred_element_type=jnp.float32
    ).astype(jnp.bfloat16)
    back = back.reshape(blocks, edge_size, feat_width)
    replies = back[0][None]
    for j in range(1, blocks):
        replies = jnp.where(selector[:, j, None, None], back[j][None], replies)
    returned = lax.all_to_all(replies, "dst", split_axis=0, concat_axis=0, tiled=True)
    src_terms = lax.dot_general(
        matrix,
        returned.reshape(masters * edge_size, feat_width),
        (((0,), (0,)), ((), ())),
        preferred_element_type=jnp.float32,
    )
    summed = scatter_sum(src_terms.reshape(holders // 2, 2, block_rows, feat_width))
    return (hidden, summed, weight_grad, bias_grad)


def solution(mesh):
    in_specs = (
        P(("src", "dst"), None),
        P("src", "dst", None, None, None),
        P("src", "dst", None),
        P("src", "dst", None),
        P("src", "dst"),
        P(),
        P(),
        P(("src", "dst"), None),
    )
    out_specs = (P(("src", "dst"), None), P(("src", "dst"), None), P(), P())
    return jax.shard_map(
        per_device, mesh=mesh, in_specs=in_specs, out_specs=out_specs, check_vma=False
    )
```

profile of v0, /device:TPU:0, one launch (start us, length us, event | category | flops | bytes accessed | tf_op | source)
XLA Modules:
  0.0 276.0 jit_solution(6293729831422772492)
XLA Ops:
  7.2 0.7 all-gather.2.cloned.1.call-update
  8.6 0.7 and_select_fusion.1
  9.4 0.7 broadcast_in_dim.76
  10.0 7.3 %all-to-all-start = ((s32[8,1,128]{2,1,0:T(1,128)}), s32[8,1,128]{2,1,0:T(1,128)S(1)}, u32[]{:S(2)}, u32[]{:S(2)}) async-start(s32[8,1,128]{2,1,0:T(1,128)} %broadcast_in_dim.76), calls=%async_computation | async-start | bytes 8192 | tf_op jit(solution)/shard_map/all_to_all | solution.py:85
  17.3 1.7 copy-done.2
  19.0 0.7 copy-done.3
  19.7 0.7 copy-done.4
  20.3 1.7 block_matrix.1
  22.0 1.3 copy-done.1
  23.4 8.6 %all-gather.2.cloned.1.call-done = bf16[1024,768]{1,0:T(8,128)(2,1)} async-done(((bf16[256,768]{1,0:T(8,128)(2,1)}), bf16[1024,768]{1,0:T(8,128)(2,1)}) %all-gather.2.cloned.1.call-update) | async-done | bytes 1572880 | tf_op jit(solution)/shard_map/all_gather | solution.py:76
  31.9 5.0 %convolution_convert_fusion.1 = bf16[1024,768]{1,0:T(8,128)(2,1)} fusion(bf16[1024,1024]{1,0:T(8,128)(2,1)} %copy-done.1, bf16[1024,768]{1,0:T(8,128)(2,1)} %all-gather.2.cloned.1.call-done), kind=kOutput, calls=%fused_computation.5 | convolution fusion | flops 1611399168 | bytes 5242880 | tf_op jit(solution)/shard_map/dot_general | solution.py:86
  36.9 5.5 %all-to-all-start.1 = ((bf16[8,128,768]{2,1,0:T(8,128)(2,1)}), bf16[8,128,768]{2,1,0:T(8,128)(2,1)S(1)}, u32[]{:S(2)}, u32[]{:S(2)}) async-start(bf16[8,128,768]{2,1,0:T(8,128)(2,1)} %bitcast.67), calls=%async_computation.1 | async-start | bytes 3145728 | tf_op jit(solution)/shard_map/all_to_all | solution.py:87
  42.6 37.3 %all-to-all-done.1 = bf16[8,128,768]{2,1,0:T(8,128)(2,1)S(1)} async-done(((bf16[8,128,768]{2,1,0:T(8,128)(2,1)}), bf16[8,128,768]{2,1,0:T(8,128)(2,1)S(1)}, u32[]{:S(2)}, u32[]{:S(2)}) %all-to-all-start.1) | async-done | bytes 1572896 | tf_op jit(solution)/shard_map/all_to_all | solution.py:87
  79.8 0.6 fusion
  80.9 1.8 fusion.12
  82.6 0.8 copy-done.6
  83.4 0.6 convolution_convert_fusion.2
  84.1 1.4 broadcast_select_fusion
  85.5 3.6 %all-to-all-start.2 = ((bf16[8,128,768]{2,1,0:T(8,128)(2,1)}), bf16[8,128,768]{2,1,0:T(8,128)(2,1)S(1)}, u32[]{:S(2)}, u32[]{:S(2)}) async-start(bf16[8,128,768]{2,1,0:T(8,128)(2,1)} %broadcast_select_fusion), calls=%async_computation.2 | async-start | bytes 3145728 | tf_op jit(solution)/shard_map/all_to_all | solution.py:128
  89.1 3.9 %copy.33 = bf16[1024,1024]{1,0:T(8,128)(2,1)} copy(bf16[1024,1024]{0,1:T(8,128)(2,1)} %bitcast.61) | data formatting | bytes 4194304 | tf_op jit(solution)/shard_map/dot_general | solution.py:129
  93.1 33.2 %all-to-all-done.2 = bf16[8,128,768]{2,1,0:T(8,128)(2,1)S(1)} async-done(((bf16[8,128,768]{2,1,0:T(8,128)(2,1)}), bf16[8,128,768]{2,1,0:T(8,128)(2,1)S(1)}, u32[]{:S(2)}, u32[]{:S(2)}) %all-to-all-start.2) | async-done | bytes 1572896 | tf_op jit(solution)/shard_map/all_to_all | solution.py:128
  126.3 3.4 %fusion.14 = f32[2,2,256,768]{3,2,1,0:T(8,128)S(1)} fusion(bf16[2,2,256,1024]{3,2,1,0:T(8,128)(2,1)} %bitcast.65, bf16[1024,768,1,1]{1,0,3,2:T(8,128)(2,1)S(1)} %bitcast.66), kind=kOutput, calls=%fused_computation.44 | convolution fusion | flops 1610612736 | bytes 6815744 | tf_op jit(solution)/shard_map/dot_general | solution.py:129
  129.9 1.2 copy-done.7
  131.1 0.6 convolution_convert_fusion
  131.7 1.3 pad_maximum_fusion
  133.1 2.4 fusion.3
  135.4 0.8 fusion.6
  136.2 0.6 collective-permute-start.1
  136.8 126.7 %all-reduce.2.cloned.1.call-done = bf16[784,1024]{1,0:T(8,128)(2,1)} async-done(((bf16[784,1024]{1,0:T(8,128)(2,1)}), bf16[784,1024]{1,0:T(8,128)(2,1)}) %all-reduce.2.cloned.1.call-update) | async-done | bytes 1605648 | tf_op jit(solution)/shard_map/psum | solution.py:118
  263.5 1.3 slice_convert_fusion.1
  264.8 3.5 %slice_convert_fusion = f32[768,1024]{1,0:T(8,128)} fusion(bf16[784,1024]{1,0:T(8,128)(2,1)} %all-reduce.2.cloned.1.call-done), kind=kLoop, calls=%fused_computation.7 | loop fusion | flops 786432 | bytes 4718592 | tf_op jit(solution)/shard_map/convert_element_type | solution.py:119
  268.3 0.8 fusion.5
  (29 shorter events, 1.0 us)
Async XLA Ops:
  7.2 73.3 %copy-start = (bf16[768,1024]{1,0:T(8,128)(2,1)S(1)}, bf16[768,1024]{1,0:T(8,128)(2,1)}, u32[]{:S(2)}) copy-start(bf16[768,1024]{1,0:T(8,128)(2,1)} %param.13) | copy-start | bytes 4718596
  7.2 24.8 %all-gather.2.cloned.1.call-start = ((), (), s32[]{:S(2)}) async-start(), calls=%async_computation.3 | async-start | bytes 1966080 | tf_op jit(solution)/shard_map/all_gather | solution.py:76
  10.0 26.9 %all-to-all-start = ((s32[8,1,128]{2,1,0:T(1,128)}), s32[8,1,128]{2,1,0:T(1,128)S(1)}, u32[]{:S(2)}, u32[]{:S(2)}) async-start(s32[8,1,128]{2,1,0:T(1,128)} %broadcast_in_dim.76), calls=%async_computation | async-start | bytes 8192 | tf_op jit(solution)/shard_map/all_to_all | solution.py:85
  17.3 1.7 copy-start.2
  19.0 0.7 copy-start.3
  19.7 0.7 copy-start.4
  22.0 1.3 copy-start.1
  36.9 42.9 %all-to-all-start.1 = ((bf16[8,128,768]{2,1,0:T(8,128)(2,1)}), bf16[8,128,768]{2,1,0:T(8,128)(2,1)S(1)}, u32[]{:S(2)}, u32[]{:S(2)}) async-start(bf16[8,128,768]{2,1,0:T(8,128)(2,1)} %bitcast.67), calls=%async_computation.1 | async-start | bytes 3145728 | tf_op jit(solution)/shard_map/all_to_all | solution.py:87
  42.4 38.0 %copy-start.9 = (f32[1024]{0:T(1024)S(1)}, f32[1024]{0:T(1024)}, u32[]{:S(2)}) copy-start(f32[1024]{0:T(1024)} %param.14) | copy-start | bytes 12292
  79.8 1.0 copy-start.8
  82.6 0.8 copy-start.6
  85.5 40.8 %all-to-all-start.2 = ((bf16[8,128,768]{2,1,0:T(8,128)(2,1)}), bf16[8,128,768]{2,1,0:T(8,128)(2,1)S(1)}, u32[]{:S(2)}, u32[]{:S(2)}) async-start(bf16[8,128,768]{2,1,0:T(8,128)(2,1)} %broadcast_select_fusion), calls=%async_computation.2 | async-start | bytes 3145728 | tf_op jit(solution)/shard_map/all_to_all | solution.py:128
  89.1 174.4 %all-reduce.2.cloned.1.call-start = ((), (), s32[]{:S(2)}) async-start(), calls=%async_computation.4 | async-start | bytes 3211264 | tf_op jit(solution)/shard_map/psum | solution.py:118
  129.7 2.0 copy-start.5
  129.7 1.4 copy-start.7
  129.8 3.2 %collective-permute-start = (bf16[2,256,768]{2,1,0:T(8,128)(2,1)S(1)}, bf16[2,256,768]{2,1,0:T(8,128)(2,1)}, u32[]{:S(2)}, u32[]{:S(2)}) collective-permute-start(bf16[2,256,768]{2,1,0:T(8,128)(2,1)S(1)} %fusion.4), channel_id=1, source_target_pairs={{0,8},{8,0},{16,24},{24,16},{1,9},{9,1},{17,25},{25,17},{2,10},{10... | collective-permute-start | bytes 2359304 | tf_op jit(solution)/shard_map/ppermute | solution.py:49
  136.2 132.1 %collective-permute-start.1 = (bf16[256,768]{1,0:T(8,128)(2,1)}, bf16[256,768]{1,0:T(8,128)(2,1)S(1)}, u32[]{:S(2)}, u32[]{:S(2)}) collective-permute-start(bf16[256,768]{1,0:T(8,128)(2,1)} %fusion.6), channel_id=1, source_target_pairs={{0,16},{8,24},{16,0},{24,8},{1,17},{9,25},{17,1},{25,9},{2,18},{10... | collective-permute-start | bytes 1179656 | tf_op jit(solution)/shard_map/ppermute | solution.py:56
Sparse Core Ops, SparseCore 0:
  9.5 22.3 all-gather.1
  133.1 130.3 all-reduce.1
where the time goes:
time: 277 us; the launch traced here: 276 us
  waiting for transfers between devices  206 us (74%)
  starting transfers between devices  17.1 us (6%)
  between operations  14.9 us (5%)
  local copies, waits for them, and re-layouts  12.3 us (4%)
  other arithmetic  12.2 us (4%)
  matrix products  11.3 us (4%)
    psum x1, waiting for transfers between devices, per_device(): reduced = lax.psum(joined, ('src', 'dst'))  127 us
    all_to_all x1, waiting for transfers between devices, per_device(): lax.all_to_all(outgoing.reshape(masters, edge_size, feat_width), 'dst', s...  37.3 us
    all_to_all x1, waiting for transfers between devices, per_device(): lax.all_to_all(replies, 'dst', split_axis=0, concat_axis=0, tiled=True)  33.2 us
    all_gather x1, waiting for transfers between devices, per_device(): column = lax.all_gather(features, 'src', axis=0, tiled=True)  8.58 us
    all_to_all x1, starting transfers between devices, per_device(): lax.all_to_all(wanted_rows, 'dst', split_axis=0, concat_axis=0, tiled=True)  7.28 us
    unnamed x20, local copies, waits for them, and re-layouts  6.72 us
  transfers between devices with their start and end apart: 7, of which 4 were waited for; matrix products, arithmetic and copies ran while one was open for 7% of the time, Pallas kernels for 1%

commit v1 on v0

v1 whole, which is shorter than its diff:
```python
import functools

import jax
import jax.numpy as jnp
from jax import lax
from jax.experimental import pallas as pl
from jax.experimental.pallas import tpu as pltpu
from jax.sharding import PartitionSpec as P

MESH = pl.DeviceIdType.MESH
CHUNKS = 3


def block_matrix_kernel(blocks, src_ref, dst_ref, count_ref, tiles_ref, out_ref, total):
    size = tiles_ref.shape[1]
    total[...] = jnp.zeros_like(total)

    def add_tile(slot, carry):
        row = pl.multiple_of(dst_ref[slot] // blocks * size, size)
        col = pl.multiple_of(src_ref[slot] * size, size)
        total[pl.ds(row, size), pl.ds(col, size)] += tiles_ref[slot].astype(jnp.float32)
        return carry

    lax.fori_loop(0, count_ref[0], add_tile, 0)
    out_ref[...] = total[...].astype(out_ref.dtype)


def block_matrix(src_ids, dst_ids, tile_total, tiles, blocks, masters, columns):
    size = tiles.shape[1]
    shape = (masters * size, columns * size)
    smem = pl.BlockSpec(memory_space=pltpu.SMEM)
    vmem = pl.BlockSpec(memory_space=pltpu.VMEM)
    held = tiles.size * 2 + shape[0] * shape[1] * 6
    return pl.pallas_call(
        lambda *refs: block_matrix_kernel(blocks, *refs),
        out_shape=jax.ShapeDtypeStruct(shape, jnp.bfloat16),
        in_specs=[smem, smem, smem, vmem],
        out_specs=vmem,
        scratch_shapes=[pltpu.VMEM(shape, jnp.float32)],
        compiler_params=pltpu.CompilerParams(vmem_limit_bytes=held + 4 * 1024 * 1024),
        cost_estimate=pl.CostEstimate(flops=tiles.size, bytes_accessed=held, transcendentals=0),
        name="block_matrix",
    )(src_ids, dst_ids, tile_total, tiles)


class Place:
    def __init__(self, sizes):
        self.sizes = sizes
        self.s = lax.axis_index("src")
        self.d = lax.axis_index("dst")
        self.at = {
            "c": lax.rem(self.s, 2),
            "y": self.s // 2,
            "x": lax.rem(self.d, sizes["x"]),
            "z": self.d // sizes["x"],
            "d": self.d,
        }

    def device(self, dim, value):
        at = dict(self.at)
        if dim == "d":
            return (self.s, value)
        at[dim] = value
        return (at["y"] * 2 + at["c"], at["z"] * self.sizes["x"] + at["x"])

    def others(self, dim):
        size = self.sizes[dim]
        return [lax.rem(self.at[dim] + step, size) for step in range(1, size)]


class Exchange:
    def __init__(self, place, dim, source, target, sent, got):
        self.place, self.dim = place, dim
        self.source, self.target, self.sent, self.got = source, target, sent, got

    def copy(self, peer, slot):
        return pltpu.make_async_remote_copy(
            src_ref=self.source(peer),
            dst_ref=self.target(slot),
            send_sem=self.sent.at[peer],
            recv_sem=self.got.at[slot],
            device_id=self.place.device(self.dim, peer),
            device_id_type=MESH,
        )

    def start(self):
        for peer in self.place.others(self.dim):
            self.copy(peer, self.place.at[self.dim]).start()

    def arrive(self):
        for peer in self.place.others(self.dim):
            self.copy(peer, peer).wait_recv()

    def drain(self):
        for peer in self.place.others(self.dim):
            self.copy(peer, peer).wait_send()


def layer_kernel(cfg, *refs):
    (
        matrix, features, weight, bias, out_grad, wanted,
        hidden, feat_grad, weight_out, bias_out,
        column, outbox, inbox, back_in, asked, flipped, agg, agg_t, grad_b, preact,
        pair, pair_out, pair_in, side_in, own_sum,
        w32, w_out, c_in, y32, y_out, y_in, x32, x_out, x_in, z32, z_out, z_in, bias_own, bias_in,
        sems,
    ) = refs
    sizes, chunks, width, size, blocks = cfg
    D, S, NY, X = sizes["d"], sizes["s"], sizes["y"], sizes["x"]
    place = Place(sizes)
    at = place.at
    rows = blocks * size
    feat = features.shape[1]
    flips = flipped is not None
    exchanges = []
    counter = [0]

    def exchange(dim, source, target):
        base = counter[0]
        counter[0] += sizes[dim]
        ex = Exchange(
            place, dim, source, target,
            sems.at[0, pl.ds(base, sizes[dim])], sems.at[1, pl.ds(base, sizes[dim])],
        )
        exchanges.append(ex)
        return ex

    barrier = pltpu.get_barrier_semaphore()
    greeted = 0
    for dim in ("d", "c", "y"):
        for peer in place.others(dim):
            pl.semaphore_signal(barrier, inc=1, device_id=place.device(dim, peer), device_id_type=MESH)
            greeted += 1
    pl.semaphore_wait(barrier, greeted)

    def part(f):
        return slice(f * width, (f + 1) * width)

    def home(f, y, c):
        return column.at[f, y, c]

    gather_y = [
        exchange("y", lambda v, f=f: features.at[:, part(f)], lambda v, f=f: home(f, v, at["c"]))
        for f in range(chunks)
    ]
    gather_c = [
        exchange("c", lambda v, f=f: features.at[:, part(f)], lambda v, f=f: home(f, at["y"], v))
        for f in range(chunks)
    ]
    passed = []
    for f in range(chunks):
        gather_y[f].start()
        gather_c[f].start()
    selectors = exchange("d", lambda v: wanted.at[v], lambda v: asked.at[v])
    selectors.start()
    asked[at["d"]] = wanted[at["d"]]
    for f in range(chunks):
        column[f, at["y"], at["c"]] = features[:, part(f)]

    step = min(D * size, 1024)

    def product(f):
        col = column[f].reshape(S * rows, width)

        def some(r, carry):
            begin = pl.multiple_of(r * step, step)
            value = jnp.dot(matrix[pl.ds(begin, step), :], col, preferred_element_type=jnp.float32)
            outbox[f, pl.ds(r * (step // size), step // size)] = value.astype(jnp.bfloat16).reshape(
                step // size, size, width
            )
            return carry

        if D * size == step:
            some(0, 0)
        else:
            lax.fori_loop(0, D * size // step, some, 0)

    forth = []
    for f in range(chunks):
        gather_y[f].arrive()
        relays = [
            exchange(
                "c",
                lambda v, f=f, o=o: home(f, o, at["c"]),
                lambda v, f=f, o=o: home(f, o, v),
            )
            for o in place.others("y")
        ]
        for relay in relays:
            relay.start()
        gather_c[f].arrive()
        for relay in relays:
            relay.arrive()
        product(f)
        ex = exchange("d", lambda v, f=f: outbox.at[f, v], lambda v, f=f: inbox.at[f, v])
        ex.start()
        forth.append(ex)
        inbox[f, at["d"]] = outbox[f, at["d"]]

    if flips:
        for r in range(D):
            flipped[:, r * size:(r + 1) * size] = matrix[r * size:(r + 1) * size, :].T

    selectors.arrive()
    for f in range(chunks):
        forth[f].arrive()
        for j in range(blocks):
            def add(k, total, j=j, f=f):
                mine = jnp.broadcast_to(asked[k, 0:1, :], (size, width)) == j
                return total + jnp.where(mine, inbox[f, k].astype(jnp.float32), 0.0)

            total = lax.fori_loop(0, D, add, jnp.zeros((size, width), jnp.float32), unroll=D <= 8)
            agg[j * size:(j + 1) * size, part(f)] = total.astype(jnp.bfloat16)
        term = jnp.dot(agg[:, part(f)], weight[part(f), :], preferred_element_type=jnp.float32)
        if f == 0:
            preact[...] = term + bias[...]
        else:
            preact[...] += term

    value = preact[...]
    gate = jax.nn.sigmoid(value)
    hidden[...] = (value * gate).astype(hidden.dtype)
    pre_grad = out_grad[...].astype(jnp.float32) * (gate * (1.0 + value * (1.0 - gate)))
    bias_row = jnp.sum(pre_grad, axis=0, keepdims=True)
    grad_b[...] = pre_grad.astype(jnp.bfloat16)
    cells = bias_own.shape[2]
    for r in range(8):
        bias_own[0, r:r + 1, :] = bias_row[:, r * cells:(r + 1) * cells]

    for ex in forth:
        ex.drain()
        exchanges.remove(ex)

    back_ex = []
    for f in range(chunks):
        back = lax.dot_general(
            grad_b[...], weight[part(f), :], (((1,), (1,)), ((), ())), preferred_element_type=jnp.float32
        ).astype(jnp.bfloat16)

        def reply(k, carry, f=f, back=back):
            chosen = jnp.broadcast_to(asked[k, 0:1, :], (size, width))
            value = back[:size].astype(jnp.float32)
            for j in range(1, blocks):
                value = jnp.where(chosen == j, back[j * size:(j + 1) * size].astype(jnp.float32), value)
            outbox[f, k] = value.astype(jnp.bfloat16)
            return carry

        lax.fori_loop(0, D, reply, 0, unroll=D <= 8)
        ex = exchange("d", lambda v, f=f: outbox.at[f, v], lambda v, f=f: back_in.at[f, v])
        ex.start()
        back_ex.append(ex)
        back_in[f, at["d"]] = outbox[f, at["d"]]

    agg_t[...] = agg[...].T
    w32[...] = jnp.dot(agg_t[...], grad_b[...], preferred_element_type=jnp.float32)
    lump = w_out.shape[3]

    def w_rows(c, y, x):
        begin = ((c * NY + y) * X + x) * lump
        return pl.ds(pl.multiple_of(begin, 8), lump)

    for c in range(2):
        for y in range(NY):
            for x in range(X):
                w_out[c, y, x] = w32[w_rows(c, y, x), :].astype(jnp.bfloat16)
    spot = [0]

    def bias_exchange(dim, stage):
        base = spot[0]
        spot[0] += sizes[dim]
        return exchange(dim, lambda v: bias_own.at[stage], lambda v: bias_in.at[base + v]), base

    def bias_add(dim, stage, base):
        total = bias_own[stage]
        for peer in place.others(dim):
            total = total + bias_in[base + peer]
        bias_own[stage + 1] = total

    columns = z_in.shape[2]

    def z_part(v):
        return pl.ds(pl.multiple_of(v * columns, 128), columns)

    def reduce_steps():
        ex = exchange("c", lambda v: w_out.at[v], lambda v: c_in)
        bx, base = bias_exchange("c", 0)
        ex.start()
        bx.start()
        yield
        ex.arrive()
        bx.arrive()
        bias_add("c", 0, base)
        for y in range(NY):
            for x in range(X):
                value = w32[w_rows(at["c"], y, x), :] + c_in[y, x].astype(jnp.float32)
                y32[y, x] = value
                y_out[y, x] = value.astype(jnp.bfloat16)
        ex = exchange("y", lambda v: y_out.at[v], lambda v: y_in.at[v])
        bx, base = bias_exchange("y", 1)
        ex.start()
        bx.start()
        yield
        ex.arrive()
        bx.arrive()
        bias_add("y", 1, base)
        for x in range(X):
            value = y32[at["y"], x]
            for o in place.others("y"):
                value = value + y_in[o, x].astype(jnp.float32)
            x32[x] = value
            x_out[x] = value.astype(jnp.bfloat16)
        ex = exchange("x", lambda v: x_out.at[v], lambda v: x_in.at[v])
        bx, base = bias_exchange("x", 2)
        ex.start()
        bx.start()
        yield
        ex.arrive()
        bx.arrive()
        bias_add("x", 2, base)
        value = x32[at["x"]]
        for o in place.others("x"):
            value = value + x_in[o].astype(jnp.float32)
        z32[...] = value
        z_out[...] = value.astype(jnp.bfloat16)
        ex = exchange("z", lambda v: z_out.at[:, z_part(v)], lambda v: z_in.at[v])
        bx, base = bias_exchange("z", 3)
        ex.start()
        bx.start()
        yield
        ex.arrive()
        bx.arrive()
        bias_add("z", 3, base)
        bias_out[...] = bias_own[4]
        value = z32[:, z_part(at["z"])]
        for o in place.others("z"):
            value = value + z_in[o].astype(jnp.float32)
        mine = weight_out.at[at["c"], at["y"], at["x"]]
        weight_out[at["c"], at["y"], at["x"], :, z_part(at["z"])] = value.astype(jnp.bfloat16)
        ex = exchange("z", lambda v: mine.at[:, z_part(at["z"])], lambda v: mine.at[:, z_part(v)])
        ex.start()
        yield
        ex.arrive()
        ex = exchange("x", lambda v: mine, lambda v: weight_out.at[at["c"], at["y"], v])
        ex.start()
        yield
        ex.arrive()
        ex = exchange("y", lambda v: weight_out.at[at["c"], at["y"]], lambda v: weight_out.at[at["c"], v])
        ex.start()
        yield
        ex.arrive()
        ex = exchange("c", lambda v: weight_out.at[at["c"]], lambda v: weight_out.at[v])
        ex.start()
        yield
        ex.arrive()

    reduction = reduce_steps()
    next(reduction)
    next(reduction)
    side = []
    for f in range(chunks):
        back_ex[f].arrive()
        given = back_in[f].reshape(D * size, width)
        for s in range(S):
            if flips:
                value = jnp.dot(
                    flipped[s * rows:(s + 1) * rows, :], given, preferred_element_type=jnp.float32
                )
            else:
                value = lax.dot_general(
                    matrix[:, s * rows:(s + 1) * rows], given, (((0,), (0,)), ((), ())),
                    preferred_element_type=jnp.float32,
                )

            @pl.when(at["c"] == s % 2)
            def _(value=value, s=s):
                pair[s // 2] = value

            pair_out[f, s % 2, s // 2] = value.astype(jnp.bfloat16)
        ex = exchange("c", lambda v, f=f: pair_out.at[f, v], lambda v, f=f: pair_in.at[f])
        ex.start()
        ex.arrive()
        for y in range(NY):
            value = pair[y] + pair_in[f, y].astype(jnp.float32)
            pair_out[f, at["c"], y] = value.astype(jnp.bfloat16)
        own_sum[f] = pair[at["y"]] + pair_in[f, at["y"]].astype(jnp.float32)
        ex = exchange("y", lambda v, f=f: pair_out.at[f, at["c"], v], lambda v, f=f: side_in.at[f, v])
        ex.start()
        side.append(ex)
        next(reduction)
    for f in range(chunks):
        side[f].arrive()
        value = own_sum[f]
        for o in place.others("y"):
            value = value + side_in[f, o].astype(jnp.float32)
        feat_grad[:, part(f)] = value.astype(feat_grad.dtype)
    for _ in reduction:
        pass
    for ex in exchanges:
        ex.drain()


def fused_layer(cfg, semaphores, features, matrix, weight, bias, out_grad, wanted):
    sizes, chunks, width, size, blocks = cfg
    D, S, NY, X, Z = sizes["d"], sizes["s"], sizes["y"], sizes["x"], sizes["z"]
    rows = blocks * size
    feat, hid = weight.shape
    lump = feat // (2 * NY * X)
    bf, f32 = jnp.bfloat16, jnp.float32
    flips = matrix.size * 2 <= 8 * 1024 * 1024
    vmem = pl.BlockSpec(memory_space=pltpu.VMEM)
    scratch = [
        pltpu.VMEM((chunks, NY, 2, rows, width), bf),
        pltpu.VMEM((chunks, D, size, width), bf),
        pltpu.VMEM((chunks, D, size, width), bf),
        pltpu.VMEM((chunks, D, size, width), bf),
        pltpu.VMEM(wanted.shape, jnp.int32),
        pltpu.VMEM((matrix.shape[1], matrix.shape[0]) if flips else (16, 128), bf),
        pltpu.VMEM((rows, feat), bf),
        pltpu.VMEM((feat, rows), bf),
        pltpu.VMEM((rows, hid), bf),
        pltpu.VMEM((rows, hid), f32),
        pltpu.VMEM((NY, rows, width), f32),
        pltpu.VMEM((chunks, 2, NY, rows, width), bf),
        pltpu.VMEM((chunks, NY, rows, width), bf),
        pltpu.VMEM((chunks, NY, rows, width), bf),
        pltpu.VMEM((chunks, rows, width), f32),
        pltpu.VMEM((feat, hid), f32),
        pltpu.VMEM((2, NY, X, lump, hid), bf),
        pltpu.VMEM((NY, X, lump, hid), bf),
        pltpu.VMEM((NY, X, lump, hid), f32),
        pltpu.VMEM((NY, X, lump, hid), bf),
        pltpu.VMEM((NY, X, lump, hid), bf),
        pltpu.VMEM((X, lump, hid), f32),
        pltpu.VMEM((X, lump, hid), bf),
        pltpu.VMEM((X, lump, hid), bf),
        pltpu.VMEM((lump, hid), f32),
        pltpu.VMEM((lump, hid), bf),
        pltpu.VMEM((Z, lump, hid // Z), bf),
        pltpu.VMEM((5, 8, hid // 8), f32),
        pltpu.VMEM((2 + NY + X + Z, 8, hid // 8), f32),
        pltpu.SemaphoreType.DMA((2, semaphores)),
    ]

    def kernel(*refs):
        refs = list(refs)
        if not flips:
            refs[10 + 5] = None
        layer_kernel(cfg, *refs)

    work = 2 * rows * feat * hid * 3 + 4 * matrix.size * feat
    return pl.pallas_call(
        kernel,
        out_shape=(
            jax.ShapeDtypeStruct((rows, hid), bf),
            jax.ShapeDtypeStruct((rows, feat), bf),
            jax.ShapeDtypeStruct((2, NY, X, lump, hid), bf),
            jax.ShapeDtypeStruct((8, hid // 8), f32),
        ),
        in_specs=[vmem] * 6,
        out_specs=(vmem, vmem, vmem, vmem),
        scratch_shapes=scratch,
        compiler_params=pltpu.CompilerParams(
            collective_id=0, has_side_effects=True, vmem_limit_bytes=62 * 1024 * 1024
        ),
        cost_estimate=pl.CostEstimate(flops=work, bytes_accessed=8 * 1024 * 1024, transcendentals=rows * hid),
        name="fused_layer",
    )(matrix, features, weight, bias, out_grad, wanted)


def per_device(features, edge_tiles, tile_src, tile_dst, tile_count, weight, out_bias, out_grad):
    capacity = edge_tiles.shape[2]
    size = edge_tiles.shape[3]
    feat = features.shape[1]
    hid = weight.shape[1]
    blocks = features.shape[0] // size
    D = lax.axis_size("dst")
    S = lax.axis_size("src")
    NY = S // 2
    X = NY if D % NY == 0 else 1
    Z = D // X
    sizes = {"d": D, "s": S, "c": 2, "y": NY, "x": X, "z": Z}
    chunks = CHUNKS
    width = feat // chunks
    cfg = (sizes, chunks, width, size, blocks)
    semaphores = chunks * (2 * NY + 2 + 2 * (NY - 1) + 2 + 2 * D) + D + 4 * (2 + NY + X + Z)
    src_ids = tile_src.reshape(capacity)
    dst_ids = tile_dst.reshape(capacity)
    alive = jnp.arange(capacity, dtype=jnp.int32) < tile_count.reshape(())
    matrix = block_matrix(
        src_ids, dst_ids, tile_count.reshape(1),
        edge_tiles.reshape(capacity, size, size), blocks, D, S * blocks,
    )
    routing = (dst_ids[None, :] // blocks == jnp.arange(D, dtype=jnp.int32)[:, None]) & alive[None, :]
    chosen = jnp.max(jnp.where(routing, dst_ids[None, :] % blocks, 0), axis=1)
    wanted = jnp.broadcast_to(chosen[:, None, None], (D, 8, width))
    hidden, feat_grad, weight_part, bias_part = fused_layer(
        cfg, semaphores, features, matrix, weight, out_bias.reshape(1, hid), out_grad, wanted
    )
    weight_grad = weight_part.reshape(feat, hid).astype(jnp.float32)
    return (hidden, feat_grad, weight_grad, bias_part.reshape(hid))


def solution(mesh):
    in_specs = (
        P(("src", "dst"), None),
        P("src", "dst", None, None, None),
        P("src", "dst", None),
        P("src", "dst", None),
        P("src", "dst"),
        P(),
        P(),
        P(("src", "dst"), None),
    )
    out_specs = (P(("src", "dst"), None), P(("src", "dst"), None), P(), P())
    return jax.shard_map(
        per_device, mesh=mesh, in_specs=in_specs, out_specs=out_specs, check_vma=False
    )
```

time: 277 us -> 134 us (0.48)
  waiting for transfers between devices: 206 us -> 0 us
  Pallas kernels: 1.71 us -> 121 us
  starting transfers between devices: 17.1 us -> 0 us
  between operations: 14.9 us -> 1.34 us
  matrix products: 11.3 us -> 0 us
  other arithmetic: 12.2 us -> 4.34 us
  local copies, waits for them, and re-layouts: 12.3 us -> 7.07 us
    psum x1 -> x0, waiting for transfers between devices: 127 us -> none  [per_device(): reduced = lax.psum(joined, ('src', 'dst'))]
    pallas_call x0 -> x1, Pallas kernels: none -> 119 us  [fused_layer(): pl.pallas_call(kernel, out_shape=(jax.ShapeDtypeStruct((rows, hid), bf),...]
    all_to_all x3 -> x0, waiting for transfers between devices: 70.4 us -> none  [the longest x1 37.3 us: per_device(): lax.all_to_all(outgoing.reshape(masters, edge_size, feat_width), 'dst', s...]
    all_to_all x3 -> x0, starting transfers between devices: 16.4 us -> none  [the longest x1 7.28 us: per_device(): lax.all_to_all(wanted_rows, 'dst', split_axis=0, concat_axis=0, tiled=True)]
    dot_general x5 -> x0, matrix products: 11.3 us -> none  [the longest x1 4.98 us: per_device(): jnp.dot(matrix, column, preferred_element_type=jnp.float32)]
    all_gather x1 -> x0, waiting for transfers between devices: 8.58 us -> none  [per_device(): column = lax.all_gather(features, 'src', axis=0, tiled=True)]
    dot_general x1 -> x0, local copies, waits for them, and re-layouts: 3.94 us -> none  [per_device(): lax.dot_general(matrix, returned.reshape(masters * edge_size, feat_width)...]
    convert_element_type x4 -> x1, other arithmetic: 5.73 us -> 3.54 us  [per_device(): weight_grad = weight_part.reshape(feat, hid).astype(jnp.float32)]
  transfers between devices with their start and end apart: 7 -> 0, of which waited for: 4 -> 0; matrix products, arithmetic and copies ran while one was open for 7% -> 0% of each run, Pallas kernels for 1% -> 0%
where the time goes in v1:
time: 134 us; the launch traced here: 133 us
  Pallas kernels  121 us (90%)
  local copies, waits for them, and re-layouts  7.07 us (5%)
  other arithmetic  4.34 us (3%)
  between operations  1.34 us (1%)
    pallas_call x1, Pallas kernels, fused_layer(): pl.pallas_call(kernel, out_shape=(jax.ShapeDtypeStruct((rows, hid), bf),...  119 us
    unnamed x17, local copies, waits for them, and re-layouts  6.36 us
    convert_element_type x1, other arithmetic, per_device(): weight_grad = weight_part.reshape(feat, hid).astype(jnp.float32)  3.54 us

profile of v1, /device:TPU:0, one launch (start us, length us, event | category | flops | bytes accessed | tf_op | source)
XLA Modules:
  0.0 133.4 jit_solution(6845973618186911019)
XLA Ops:
  1.3 0.7 and_select_fusion.1
  2.0 0.1 select_reduce_fusion
  2.1 0.7 broadcast_in_dim.22.refs_5_
  2.8 0.0 copy-start
  2.8 1.6 %copy-done = bf16[1,1,64,128,128]{4,3,2,1,0:T(8,128)(2,1)S(1)} copy-done((bf16[1,1,64,128,128]{4,3,2,1,0:T(8,128)(2,1)S(1)}, bf16[1,1,64,128,128]{4,3,2,1,0:T(8,128)(2,1)}, u32[]{:S(2)}) %copy-start) | copy-done | bytes 2097176
  4.4 0.0 copy-start.2
  4.4 0.7 copy-done.2
  5.0 0.0 copy-start.3
  5.0 0.7 copy-done.3
  5.7 1.6 %block_matrix.1.refs_0_ = bf16[1024,1024]{1,0:T(8,128)(2,1)S(1)} custom-call(s32[64]{0:T(128)S(1)} %bitcast.19, s32[64]{0:T(128)S(1)} %bitcast.20, s32[1]{0:T(128)} %bitcast.16.refs_2_, bf16[64,128,128]{2,1,0:T(8,128)(2,1)S(1)} %bitcast.18), custom_call_target="tpu_custom_call" | custom-call | flops 1048576 | bytes 8388608 | tf_op jit(solution)/shard_map/block_matrix/pallas_call | solution.py:34
  7.3 0.0 copy-start.1
  7.3 1.3 copy-done.1
  8.6 119.0 %fused_layer.1 = (bf16[256,1024]{1,0:T(8,128)(2,1)}, bf16[256,768]{1,0:T(8,128)(2,1)}, bf16[2,2,2,96,1024]{4,3,2,1,0:T(8,128)(2,1)}, f32[8,128]{1,0:T(8,128)}) custom-call(bf16[1024,1024]{1,0:T(8,128)(2,1)} %copy-done.1, bf16[256,768]{1,0:T(8,128)(2,1)} %refs_1_.1, bf16[768,1024]{1,0:T(8,128)(2,1)} %refs_2_.1, f32[1,1024]{1,0:T(1,128)} %bitcast.22, ...), custom_call_target="tpu_custom_call" | custom-call | flops 4429185024 | bytes 8388608 | tf_op jit(solution)/shard_map/fused_layer/pallas_call | solution.py:451
  127.7 0.0 copy-start.4
  127.7 0.0 copy-start.5
  127.7 0.0 copy-start.6
  127.7 3.5 %bitcast_convert_fusion = f32[768,1024]{1,0:T(8,128)} fusion(bf16[2,2,2,96,1024]{4,3,2,1,0:T(8,128)(2,1)} %get-tuple-element.10), kind=kLoop, calls=%fused_computation | loop fusion | flops 786432 | bytes 4718592 | tf_op jit(solution)/shard_map/convert_element_type | solution.py:499
  131.3 0.0 copy-done.4
  131.3 0.8 copy.16
  132.1 0.0 copy-done.5
  132.1 0.7 copy.17
  132.8 0.0 copy-done.6
  132.8 0.6 copy.18
  (1 shorter events, 0.0 us)
Async XLA Ops:
  2.8 1.6 %copy-start = (bf16[1,1,64,128,128]{4,3,2,1,0:T(8,128)(2,1)S(1)}, bf16[1,1,64,128,128]{4,3,2,1,0:T(8,128)(2,1)}, u32[]{:S(2)}) copy-start(bf16[1,1,64,128,128]{4,3,2,1,0:T(8,128)(2,1)} %param.9) | copy-start | bytes 6291460
  4.4 0.7 copy-start.2
  5.0 0.7 copy-start.3
  7.3 1.3 copy-start.1
  127.7 3.6 %copy-start.4 = (bf16[256,1024]{1,0:T(8,128)(2,1)S(1)}, bf16[256,1024]{1,0:T(8,128)(2,1)}, u32[]{:S(2)}) copy-start(bf16[256,1024]{1,0:T(8,128)(2,1)} %get-tuple-element.18) | copy-start | bytes 1572868
  127.7 4.4 %copy-start.5 = (bf16[256,768]{1,0:T(8,128)(2,1)S(1)}, bf16[256,768]{1,0:T(8,128)(2,1)}, u32[]{:S(2)}) copy-start(bf16[256,768]{1,0:T(8,128)(2,1)} %get-tuple-element.19) | copy-start | bytes 1179652
  127.7 5.1 %copy-start.6 = (f32[8,128]{1,0:T(8,128)S(1)}, f32[8,128]{1,0:T(8,128)}, u32[]{:S(2)}) copy-start(f32[8,128]{1,0:T(8,128)} %get-tuple-element.11) | copy-start | bytes 12292

commit v2 on v1

--- a/solution.py
+++ b/solution.py
@@ -1,4 +1,4 @@
-import functools
+import math
 
 import jax
 import jax.numpy as jnp
@@ -8,24 +8,25 @@
 from jax.sharding import PartitionSpec as P
 
 MESH = pl.DeviceIdType.MESH
-CHUNKS = 3
-
-
-def block_matrix_kernel(blocks, src_ref, dst_ref, count_ref, tiles_ref, out_ref, total):
+
+
+def block_matrix_kernel(blocks, src_ref, dst_ref, count_ref, tiles_ref, out_ref, wanted_ref, total):
     size = tiles_ref.shape[1]
     total[...] = jnp.zeros_like(total)
+    wanted_ref[...] = jnp.zeros_like(wanted_ref)
 
     def add_tile(slot, carry):
         row = pl.multiple_of(dst_ref[slot] // blocks * size, size)
         col = pl.multiple_of(src_ref[slot] * size, size)
         total[pl.ds(row, size), pl.ds(col, size)] += tiles_ref[slot].astype(jnp.float32)
+        wanted_ref[dst_ref[slot] // blocks] = jnp.full(wanted_ref.shape[1:], dst_ref[slot] % blocks, jnp.int32)
         return carry
 
     lax.fori_loop(0, count_ref[0], add_tile, 0)
     out_ref[...] = total[...].astype(out_ref.dtype)
 
 
-def block_matrix(src_ids, dst_ids, tile_total, tiles, blocks, masters, columns):
+def block_matrix(src_ids, dst_ids, tile_total, tiles, blocks, masters, columns, width):
     size = tiles.shape[1]
     shape = (masters * size, columns * size)
     smem = pl.BlockSpec(memory_space=pltpu.SMEM)
@@ -33,9 +34,12 @@
     held = tiles.size * 2 + shape[0] * shape[1] * 6
     return pl.pallas_call(
         lambda *refs: block_matrix_kernel(blocks, *refs),
-        out_shape=jax.ShapeDtypeStruct(shape, jnp.bfloat16),
+        out_shape=(
+            jax.ShapeDtypeStruct(shape, jnp.bfloat16),
+            jax.ShapeDtypeStruct((masters, 8, width), jnp.int32),
+        ),
         in_specs=[smem, smem, smem, vmem],
-        out_specs=vmem,
+        out_specs=(vmem, vmem),
         scratch_shapes=[pltpu.VMEM(shape, jnp.float32)],
         compiler_params=pltpu.CompilerParams(vmem_limit_bytes=held + 4 * 1024 * 1024),
         cost_estimate=pl.CostEstimate(flops=tiles.size, bytes_accessed=held, transcendentals=0),
@@ -103,9 +107,10 @@
         column, outbox, inbox, back_in, asked, flipped, agg, agg_t, grad_b, preact,
         pair, pair_out, pair_in, side_in, own_sum,
         w32, w_out, c_in, y32, y_out, y_in, x32, x_out, x_in, z32, z_out, z_in, bias_own, bias_in,
+        relay_in, relay_asked, relay_sum, relay_got, relay_out, gathered,
         sems,
     ) = refs
-    sizes, chunks, width, size, blocks = cfg
+    sizes, chunks, width, size, blocks, halves, relayed = cfg
     D, S, NY, X = sizes["d"], sizes["s"], sizes["y"], sizes["x"]
     place = Place(sizes)
     at = place.at
@@ -115,15 +120,22 @@
     exchanges = []
     counter = [0]
 
+    def grab(count):
+        base = counter[0]
+        counter[0] += count
+        return sems.at[0, pl.ds(base, count)], sems.at[1, pl.ds(base, count)]
+
     def exchange(dim, source, target):
-        base = counter[0]
-        counter[0] += sizes[dim]
-        ex = Exchange(
-            place, dim, source, target,
-            sems.at[0, pl.ds(base, sizes[dim])], sems.at[1, pl.ds(base, sizes[dim])],
-        )
+        sent, got = grab(sizes[dim])
+        ex = Exchange(place, dim, source, target, sent, got)
         exchanges.append(ex)
         return ex
+
+    def wire(source, target, sent, got, device):
+        return pltpu.make_async_remote_copy(
+            src_ref=source, dst_ref=target, send_sem=sent, recv_sem=got,
+            device_id=device, device_id_type=MESH,
+        )
 
     barrier = pltpu.get_barrier_semaphore()
     greeted = 0
@@ -175,6 +187,277 @@
         else:
             lax.fori_loop(0, D * size // step, some, 0)
 
+
+    Z = sizes["z"]
+    everyone = range(X)
+    beside = [lax.rem(at["x"] + step, X) for step in range(1, X)]
+    half = at["z"] // 2
+    inner = (at["z"] == 1) | (at["z"] == 2)
+    edge = jnp.logical_not(inner)
+    near_inner, far_inner = 1 + half, 2 - half
+    near_edge, far_edge = 3 * half, 3 - 3 * half
+    other = near_edge + near_inner - at["z"]
+    rank = jnp.where(inner, 1, 0)
+
+    def spot_of(z, x):
+        return z * X + x
+
+    def here(z, x):
+        return (at["y"] * 2 + at["c"], spot_of(z, x))
+
+    def close_pairs():
+        return [(other, x) for x in everyone] + [(at["z"], x) for x in beside]
+
+    def sender_pairs():
+        return close_pairs() + [(far_inner, x) for x in everyone]
+
+    def far_pairs():
+        return [(far_inner, x) for x in everyone] + [(far_edge, x) for x in everyone]
+
+    def via_pairs(act):
+        for x in beside:
+            act(x)
+
+        @pl.when(edge)
+        def _():
+            act(at["x"])
+
+    def sources_at_relay(act):
+        for x in everyone:
+            act(0, x)
+        for x in beside:
+            act(1, x)
+
+    class Forth:
+        def __init__(self, f):
+            self.f = f
+            self.sent, self.got = grab(D)
+            self.up_sent, self.up_got = grab(2 * X)
+            self.sum_sent, self.sum_got = grab(1)
+
+        def direct(self, z, x):
+            m = spot_of(z, x)
+            return wire(outbox.at[self.f, m], inbox.at[self.f, at["d"]], self.sent.at[m], self.got.at[at["d"]], here(z, x))
+
+        def up(self, x):
+            return wire(
+                outbox.at[self.f, spot_of(far_edge, x)], relay_in.at[self.f, rank * X + at["x"]],
+                self.up_sent.at[x], self.up_got.at[rank * X + at["x"]], here(near_inner, x),
+            )
+
+        def total(self):
+            return wire(
+                relay_sum.at[self.f], relay_got.at[self.f], self.sum_sent.at[0], self.sum_got.at[0],
+                here(far_edge, at["x"]),
+            )
+
+        def start(self):
+            via_pairs(lambda x: self.up(x).start())
+            for z, x in [(far_inner, x) for x in everyone] + close_pairs():
+                self.direct(z, x).start()
+
+        def relay(self):
+            f = self.f
+
+            @pl.when(inner)
+            def _():
+                def wait(who, x):
+                    slot = who * X + x
+                    ref = relay_in.at[f, slot]
+                    wire(ref, ref, self.up_sent.at[0], self.up_got.at[slot], here(far_edge, at["x"])).wait_recv()
+
+                sources_at_relay(wait)
+                mine = outbox[f, spot_of(far_edge, at["x"])].astype(jnp.float32)
+                chosen = jnp.broadcast_to(wanted[spot_of(far_edge, at["x"]), 0:1, :], (size, width))
+                totals = [jnp.where(chosen == j, mine, 0.0) for j in range(blocks)]
+
+                def add(who, x):
+                    slot = who * X + x
+                    value = relay_in[f, slot].astype(jnp.float32)
+                    chosen = jnp.broadcast_to(relay_asked[slot, 0:1, :], (size, width))
+                    for j in range(blocks):
+                        totals[j] = totals[j] + jnp.where(chosen == j, value, 0.0)
+
+                sources_at_relay(add)
+                for j in range(blocks):
+                    relay_sum[f, j] = totals[j].astype(jnp.bfloat16)
+                self.total().start()
+
+        def finish(self):
+            f = self.f
+
+            def wait(z, x):
+                k = spot_of(z, x)
+                ref = inbox.at[f, k]
+                wire(ref, ref, self.sent.at[k], self.got.at[k], here(z, x)).wait_recv()
+
+            def masked(k, j):
+                mine = jnp.broadcast_to(asked[k, 0:1, :], (size, width)) == j
+                return jnp.where(mine, inbox[f, k].astype(jnp.float32), 0.0)
+
+            for z, x in close_pairs():
+                wait(z, x)
+            for j in range(blocks):
+                value = masked(at["d"], j)
+                for z, x in close_pairs():
+                    value = value + masked(spot_of(z, x), j)
+                gathered[j] = value
+
+            @pl.when(inner)
+            def _():
+                for z, x in far_pairs():
+                    wait(z, x)
+                for j in range(blocks):
+                    value = gathered[j]
+                    for z, x in far_pairs():
+                        value = value + masked(spot_of(z, x), j)
+                    gathered[j] = value
+
+            @pl.when(edge)
+            def _():
+                ref = relay_got.at[f]
+                wire(ref, ref, self.sum_sent.at[0], self.sum_got.at[0], here(far_inner, at["x"])).wait_recv()
+                for j in range(blocks):
+                    gathered[j] += relay_got[f, j].astype(jnp.float32)
+
+            for j in range(blocks):
+                agg[j * size:(j + 1) * size, part(f)] = gathered[j].astype(jnp.bfloat16)
+
+        def drain(self):
+            via_pairs(lambda x: self.up(x).wait_send())
+            for z, x in sender_pairs():
+                self.direct(z, x).wait_send()
+
+            @pl.when(inner)
+            def _():
+                self.total().wait_send()
+
+    class Back:
+        def __init__(self, f):
+            self.f = f
+            self.sent, self.got = grab(D)
+            self.both_sent, self.both_got = grab(1)
+            self.down_sent, _ = grab(2 * X)
+
+        def direct(self, z, x):
+            k = spot_of(z, x)
+            return wire(outbox.at[self.f, k], back_in.at[self.f, at["d"]], self.sent.at[k], self.got.at[at["d"]], here(z, x))
+
+        def both(self):
+            return wire(
+                relay_sum.at[self.f], relay_got.at[self.f], self.both_sent.at[0], self.both_got.at[0],
+                here(far_inner, at["x"]),
+            )
+
+        def down(self, who, x):
+            slot = who * X + x
+            m = spot_of(far_edge, at["x"])
+            z = near_inner if who else near_edge
+            return wire(relay_out.at[self.f, slot], back_in.at[self.f, m], self.down_sent.at[slot], self.got.at[m], here(z, x))
+
+        def start(self, back):
+            f = self.f
+
+            @pl.when(edge)
+            def _():
+                for j in range(blocks):
+                    relay_sum[f, j] = back[j * size:(j + 1) * size]
+                self.both().start()
+
+            def reply(k):
+                chosen = jnp.broadcast_to(asked[k, 0:1, :], (size, width))
+                value = back[:size].astype(jnp.float32)
+                for j in range(1, blocks):
+                    value = jnp.where(chosen == j, back[j * size:(j + 1) * size].astype(jnp.float32), value)
+                return value.astype(jnp.bfloat16)
+
+            @pl.when(inner)
+            def _():
+                for z, x in far_pairs():
+                    outbox[f, spot_of(z, x)] = reply(spot_of(z, x))
+                    self.direct(z, x).start()
+
+            for z, x in close_pairs():
+                outbox[f, spot_of(z, x)] = reply(spot_of(z, x))
+                self.direct(z, x).start()
+            back_in[f, at["d"]] = reply(at["d"])
+
+        def relay(self):
+            f = self.f
+
+            @pl.when(inner)
+            def _():
+                ref = relay_got.at[f]
+                wire(ref, ref, self.both_sent.at[0], self.both_got.at[0], here(far_edge, at["x"])).wait_recv()
+
+                def pick(table):
+                    chosen = jnp.broadcast_to(table, (size, width))
+                    value = relay_got[f, 0].astype(jnp.float32)
+                    for j in range(1, blocks):
+                        value = jnp.where(chosen == j, relay_got[f, j].astype(jnp.float32), value)
+                    return value.astype(jnp.bfloat16)
+
+                def pass_on(who, x):
+                    slot = who * X + x
+                    relay_out[f, slot] = pick(relay_asked[slot, 0:1, :])
+                    self.down(who, x).start()
+
+                sources_at_relay(pass_on)
+                m = spot_of(far_edge, at["x"])
+                back_in[f, m] = pick(wanted[m, 0:1, :])
+
+        def arrive(self):
+            def wait(z, x):
+                k = spot_of(z, x)
+                ref = back_in.at[self.f, k]
+                wire(ref, ref, self.sent.at[k], self.got.at[k], here(z, x)).wait_recv()
+
+            for z, x in sender_pairs():
+                wait(z, x)
+
+            def from_relay(x):
+                k = spot_of(far_edge, x)
+                ref = back_in.at[self.f, k]
+                wire(ref, ref, self.sent.at[k], self.got.at[k], here(far_edge, x)).wait_recv()
+
+            via_pairs(from_relay)
+
+        def drain(self):
+            for z, x in close_pairs():
+                self.direct(z, x).wait_send()
+
+            @pl.when(inner)
+            def _():
+                for z, x in far_pairs():
+                    self.direct(z, x).wait_send()
+                sources_at_relay(lambda who, x: self.down(who, x).wait_send())
+
+            @pl.when(edge)
+            def _():
+                self.both().wait_send()
+
+    if relayed:
+        ask_sent, ask_got = grab(2 * X)
+
+        def ask(x):
+            slot = rank * X + at["x"]
+            return wire(
+                wanted.at[spot_of(far_edge, x)], relay_asked.at[slot], ask_sent.at[x], ask_got.at[slot],
+                here(near_inner, x),
+            )
+
+        via_pairs(lambda x: ask(x).start())
+
+    def asked_at_relay():
+        @pl.when(inner)
+        def _():
+            def wait(who, x):
+                slot = who * X + x
+                ref = relay_asked.at[slot]
+                wire(ref, ref, ask_sent.at[0], ask_got.at[slot], here(far_edge, at["x"])).wait_recv()
+
+            sources_at_relay(wait)
+
     forth = []
     for f in range(chunks):
         gather_y[f].arrive()
@@ -192,10 +475,18 @@
         for relay in relays:
             relay.arrive()
         product(f)
-        ex = exchange("d", lambda v, f=f: outbox.at[f, v], lambda v, f=f: inbox.at[f, v])
+        if relayed:
+            ex = Forth(f)
+            exchanges.append(ex)
+        else:
+            ex = exchange("d", lambda v, f=f: outbox.at[f, v], lambda v, f=f: inbox.at[f, v])
         ex.start()
         forth.append(ex)
         inbox[f, at["d"]] = outbox[f, at["d"]]
+        if relayed and f == 1:
+            asked_at_relay()
+        if relayed and f >= 2:
+            forth[f - 2].relay()
 
     if flips:
         for r in range(D):
@@ -203,8 +494,14 @@
 
     selectors.arrive()
     for f in range(chunks):
-        forth[f].arrive()
-        for j in range(blocks):
+        if relayed:
+            for ahead in range(chunks - 2, chunks):
+                if ahead == f + 1 or (f == 0 and ahead <= f + 1):
+                    forth[ahead].relay()
+            forth[f].finish()
+        else:
+            forth[f].arrive()
+        for j in range(0 if relayed else blocks):
             def add(k, total, j=j, f=f):
                 mine = jnp.broadcast_to(asked[k, 0:1, :], (size, width)) == j
                 return total + jnp.where(mine, inbox[f, k].astype(jnp.float32), 0.0)
@@ -237,6 +534,13 @@
             grad_b[...], weight[part(f), :], (((1,), (1,)), ((), ())), preferred_element_type=jnp.float32
         ).astype(jnp.bfloat16)
 
+        if relayed:
+            ex = Back(f)
+            exchanges.append(ex)
+            ex.start(back)
+            back_ex.append(ex)
+            continue
+
         def reply(k, carry, f=f, back=back):
             chosen = jnp.broadcast_to(asked[k, 0:1, :], (size, width))
             value = back[:size].astype(jnp.float32)
@@ -254,15 +558,16 @@
     agg_t[...] = agg[...].T
     w32[...] = jnp.dot(agg_t[...], grad_b[...], preferred_element_type=jnp.float32)
     lump = w_out.shape[3]
-
-    def w_rows(c, y, x):
-        begin = ((c * NY + y) * X + x) * lump
-        return pl.ds(pl.multiple_of(begin, 8), lump)
-
-    for c in range(2):
-        for y in range(NY):
-            for x in range(X):
-                w_out[c, y, x] = w32[w_rows(c, y, x), :].astype(jnp.bfloat16)
+    wide = weight_out.shape[4]
+    span = wide // halves
+    columns = span // Z
+
+    def cols(h):
+        return slice(h * span, (h + 1) * span)
+
+    def z_part(h, v):
+        return pl.ds(pl.multiple_of(h * span + v * columns, 128), columns)
+
     spot = [0]
 
     def bias_exchange(dim, stage):
@@ -276,88 +581,95 @@
             total = total + bias_in[base + peer]
         bias_own[stage + 1] = total
 
-    columns = z_in.shape[2]
-
-    def z_part(v):
-        return pl.ds(pl.multiple_of(v * columns, 128), columns)
-
-    def reduce_steps():
-        ex = exchange("c", lambda v: w_out.at[v], lambda v: c_in)
-        bx, base = bias_exchange("c", 0)
-        ex.start()
-        bx.start()
+    def reduce_steps(h, a, b):
+        A, B, own = sizes[a], sizes[b], cols(h)
+        me_a, me_b, me_c = at[a], at[b], at["c"]
+        bias_too = h == 0
+
+        def w_rows(c, i, j):
+            return pl.ds(pl.multiple_of(((c * A + i) * B + j) * lump, 8), lump)
+
+        def begin(dim, stage, source, target):
+            ex = exchange(dim, source, target)
+            ex.start()
+            if bias_too:
+                bx, base = bias_exchange(dim, stage)
+                bx.start()
+            return lambda: (ex.arrive(), bias_too and (bx.arrive(), bias_add(dim, stage, base)))
+
+        for c in range(2):
+            for i in range(A):
+                for j in range(B):
+                    w_out[c, i, j, :, own] = w32[w_rows(c, i, j), own].astype(jnp.bfloat16)
+        end = begin("c", 0, lambda v: w_out.at[v, :, :, :, own], lambda v: c_in.at[:, :, :, own])
         yield
-        ex.arrive()
-        bx.arrive()
-        bias_add("c", 0, base)
-        for y in range(NY):
-            for x in range(X):
-                value = w32[w_rows(at["c"], y, x), :] + c_in[y, x].astype(jnp.float32)
-                y32[y, x] = value
-                y_out[y, x] = value.astype(jnp.bfloat16)
-        ex = exchange("y", lambda v: y_out.at[v], lambda v: y_in.at[v])
-        bx, base = bias_exchange("y", 1)
-        ex.start()
-        bx.start()
+        end()
+        for i in range(A):
+            for j in range(B):
+                value = w32[w_rows(me_c, i, j), own] + c_in[i, j, :, own].astype(jnp.float32)
+                y32[i, j, :, own] = value
+                y_out[i, j, :, own] = value.astype(jnp.bfloat16)
+        end = begin(a, 1, lambda v: y_out.at[v, :, :, own], lambda v: y_in.at[v, :, :, own])
         yield
-        ex.arrive()
-        bx.arrive()
-        bias_add("y", 1, base)
-        for x in range(X):
-            value = y32[at["y"], x]
-            for o in place.others("y"):
-                value = value + y_in[o, x].astype(jnp.float32)
-            x32[x] = value
-            x_out[x] = value.astype(jnp.bfloat16)
-        ex = exchange("x", lambda v: x_out.at[v], lambda v: x_in.at[v])
-        bx, base = bias_exchange("x", 2)
-        ex.start()
-        bx.start()
+        end()
+        for j in range(B):
+            value = y32[me_a, j, :, own]
+            for o in place.others(a):
+                value = value + y_in[o, j, :, own].astype(jnp.float32)
+            x32[j, :, own] = value
+            x_out[j, :, own] = value.astype(jnp.bfloat16)
+        end = begin(b, 2, lambda v: x_out.at[v, :, own], lambda v: x_in.at[v, :, own])
         yield
-        ex.arrive()
-        bx.arrive()
-        bias_add("x", 2, base)
-        value = x32[at["x"]]
-        for o in place.others("x"):
-            value = value + x_in[o].astype(jnp.float32)
-        z32[...] = value
-        z_out[...] = value.astype(jnp.bfloat16)
-        ex = exchange("z", lambda v: z_out.at[:, z_part(v)], lambda v: z_in.at[v])
-        bx, base = bias_exchange("z", 3)
-        ex.start()
-        bx.start()
+        end()
+        value = x32[me_b, :, own]
+        for o in place.others(b):
+            value = value + x_in[o, :, own].astype(jnp.float32)
+        z32[:, own] = value
+        z_out[:, own] = value.astype(jnp.bfloat16)
+        end = begin("z", 3, lambda v: z_out.at[:, z_part(h, v)], lambda v: z_in.at[h, v])
         yield
-        ex.arrive()
-        bx.arrive()
-        bias_add("z", 3, base)
-        bias_out[...] = bias_own[4]
-        value = z32[:, z_part(at["z"])]
+        end()
+        value = z32[:, z_part(h, at["z"])]
         for o in place.others("z"):
-            value = value + z_in[o].astype(jnp.float32)
-        mine = weight_out.at[at["c"], at["y"], at["x"]]
-        weight_out[at["c"], at["y"], at["x"], :, z_part(at["z"])] = value.astype(jnp.bfloat16)
-        ex = exchange("z", lambda v: mine.at[:, z_part(at["z"])], lambda v: mine.at[:, z_part(v)])
+            value = value + z_in[h, o].astype(jnp.float32)
+        if bias_too:
+            bias_out[...] = bias_own[4]
+        mine = weight_out.at[me_c, me_a, me_b]
+        weight_out[me_c, me_a, me_b, :, z_part(h, at["z"])] = value.astype(jnp.bfloat16)
+        ex = exchange("z", lambda v: mine.at[:, z_part(h, at["z"])], lambda v: mine.at[:, z_part(h, v)])
         ex.start()
         yield
         ex.arrive()
-        ex = exchange("x", lambda v: mine, lambda v: weight_out.at[at["c"], at["y"], v])
+        ex = exchange(b, lambda v: mine.at[:, own], lambda v: weight_out.at[me_c, me_a, v, :, own])
         ex.start()
         yield
         ex.arrive()
-        ex = exchange("y", lambda v: weight_out.at[at["c"], at["y"]], lambda v: weight_out.at[at["c"], v])
+        ex = exchange(
+            a, lambda v: weight_out.at[me_c, me_a, :, :, own], lambda v: weight_out.at[me_c, v, :, :, own]
+        )
         ex.start()
         yield
         ex.arrive()
-        ex = exchange("c", lambda v: weight_out.at[at["c"]], lambda v: weight_out.at[v])
+        ex = exchange("c", lambda v: weight_out.at[me_c, :, :, :, own], lambda v: weight_out.at[v, :, :, :, own])
         ex.start()
         yield
         ex.arrive()
 
-    reduction = reduce_steps()
-    next(reduction)
-    next(reduction)
+    reductions = [reduce_steps(h, *("yx" if h == 0 else "xy")) for h in range(halves)]
+
+    def advance():
+        for reduction in reductions:
+            next(reduction, None)
+
+    advance()
+    advance()
+    stages = -(-6 // chunks)
     side = []
     for f in range(chunks):
+        if relayed:
+            for ahead in ([0, 1] if f == 0 else [f + 1]):
+                if ahead < chunks:
+                    back_ex[ahead].relay()
         back_ex[f].arrive()
         given = back_in[f].reshape(D * size, width)
         for s in range(S):
@@ -386,21 +698,25 @@
         ex = exchange("y", lambda v, f=f: pair_out.at[f, at["c"], v], lambda v, f=f: side_in.at[f, v])
         ex.start()
         side.append(ex)
-        next(reduction)
+        for _ in range(stages):
+            advance()
     for f in range(chunks):
         side[f].arrive()
         value = own_sum[f]
         for o in place.others("y"):
             value = value + side_in[f, o].astype(jnp.float32)
         feat_grad[:, part(f)] = value.astype(feat_grad.dtype)
-    for _ in reduction:
-        pass
+    for reduction in reductions:
+        for _ in reduction:
+            pass
     for ex in exchanges:
         ex.drain()
+    if relayed:
+        via_pairs(lambda x: ask(x).wait_send())
 
 
 def fused_layer(cfg, semaphores, features, matrix, weight, bias, out_grad, wanted):
-    sizes, chunks, width, size, blocks = cfg
+    sizes, chunks, width, size, blocks, halves, relayed = cfg
     D, S, NY, X, Z = sizes["d"], sizes["s"], sizes["y"], sizes["x"], sizes["z"]
     rows = blocks * size
     feat, hid = weight.shape
@@ -435,11 +751,21 @@
         pltpu.VMEM((X, lump, hid), bf),
         pltpu.VMEM((lump, hid), f32),
         pltpu.VMEM((lump, hid), bf),
-        pltpu.VMEM((Z, lump, hid // Z), bf),
+        pltpu.VMEM((halves, Z, lump, hid // halves // Z), bf),
         pltpu.VMEM((5, 8, hid // 8), f32),
         pltpu.VMEM((2 + NY + X + Z, 8, hid // 8), f32),
+        pltpu.VMEM((chunks, 2 * X, size, width) if relayed else (1, 1, 16, 128), bf),
+        pltpu.VMEM((2 * X, 8, width), jnp.int32),
+        pltpu.VMEM((chunks, blocks, size, width) if relayed else (1, 1, 16, 128), bf),
+        pltpu.VMEM((chunks, blocks, size, width) if relayed else (1, 1, 16, 128), bf),
+        pltpu.VMEM((chunks, 2 * X, size, width) if relayed else (1, 1, 16, 128), bf),
+        pltpu.VMEM((blocks, size, width) if relayed else (1, 8, 128), f32),
         pltpu.SemaphoreType.DMA((2, semaphores)),
     ]
+
+    held = sum(math.prod(s.shape) * s.dtype.itemsize for s in scratch[:-1])
+    held += sum(x.size * x.dtype.itemsize for x in (features, matrix, weight, bias, out_grad, wanted))
+    held += rows * (hid + feat) * 2 + feat * hid * 3
 
     def kernel(*refs):
         refs = list(refs)
@@ -460,7 +786,7 @@
         out_specs=(vmem, vmem, vmem, vmem),
         scratch_shapes=scratch,
         compiler_params=pltpu.CompilerParams(
-            collective_id=0, has_side_effects=True, vmem_limit_bytes=62 * 1024 * 1024
+            collective_id=0, has_side_effects=True, vmem_limit_bytes=min(held + 8 * 1024 * 1024, 63 * 1024 * 1024)
         ),
         cost_estimate=pl.CostEstimate(flops=work, bytes_accessed=8 * 1024 * 1024, transcendentals=rows * hid),
         name="fused_layer",
@@ -479,20 +805,20 @@
     X = NY if D % NY == 0 else 1
     Z = D // X
     sizes = {"d": D, "s": S, "c": 2, "y": NY, "x": X, "z": Z}
-    chunks = CHUNKS
+    chunks = feat // 128 if D <= 8 else feat // 256
+    halves = 2 if NY == X and hid % (256 * Z) == 0 else 1
+    relayed = Z == 4
     width = feat // chunks
-    cfg = (sizes, chunks, width, size, blocks)
-    semaphores = chunks * (2 * NY + 2 + 2 * (NY - 1) + 2 + 2 * D) + D + 4 * (2 + NY + X + Z)
+    cfg = (sizes, chunks, width, size, blocks, halves, relayed)
+    semaphores = chunks * (2 * NY + 2 + 2 * (NY - 1) + 2 + 2 * D) + D + (2 * halves + 2) * (2 + NY + X + Z)
+    if relayed:
+        semaphores += chunks * (4 * X + 2) + 2 * X
     src_ids = tile_src.reshape(capacity)
     dst_ids = tile_dst.reshape(capacity)
-    alive = jnp.arange(capacity, dtype=jnp.int32) < tile_count.reshape(())
-    matrix = block_matrix(
+    matrix, wanted = block_matrix(
         src_ids, dst_ids, tile_count.reshape(1),
-        edge_tiles.reshape(capacity, size, size), blocks, D, S * blocks,
+        edge_tiles.reshape(capacity, size, size), blocks, D, S * blocks, width,
     )
-    routing = (dst_ids[None, :] // blocks == jnp.arange(D, dtype=jnp.int32)[:, None]) & alive[None, :]
-    chosen = jnp.max(jnp.where(routing, dst_ids[None, :] % blocks, 0), axis=1)
-    wanted = jnp.broadcast_to(chosen[:, None, None], (D, 8, width))
     hidden, feat_grad, weight_part, bias_part = fused_layer(
         cfg, semaphores, features, matrix, weight, out_bias.reshape(1, hid), out_grad, wanted
     )

time: 134 us -> 105 us (0.78)
  Pallas kernels: 121 us -> 95.5 us
  other arithmetic: 4.34 us -> 2.16 us
    pallas_call x1, Pallas kernels: 119 us -> 94.1 us  [fused_layer(): pl.pallas_call(kernel, out_shape=(jax.ShapeDtypeStruct((rows, hid), bf),...]
    convert_element_type x1, other arithmetic: 3.54 us -> 2.16 us  [per_device(): weight_grad = weight_part.reshape(feat, hid).astype(jnp.float32)]
where the time goes in v2:
time: 105 us
  Pallas kernels  95.5 us (91%)
  local copies, waits for them, and re-layouts  6.08 us (6%)
  other arithmetic  2.16 us (2%)
  between operations  1.35 us (1%)
    pallas_call x1, Pallas kernels, fused_layer(): pl.pallas_call(kernel, out_shape=(jax.ShapeDtypeStruct((rows, hid), bf),...  94.1 us
    unnamed x17, local copies, waits for them, and re-layouts  6.08 us
    convert_element_type x1, other arithmetic, per_device(): weight_grad = weight_part.reshape(feat, hid).astype(jnp.float32)  2.16 us

profile of v2, /device:TPU:0, one launch (start us, length us, event | category | flops | bytes accessed | tf_op | source)
XLA Modules:
  0.0 105.1 jit_solution(2384973999390361045)
XLA Ops:
  0.6 0.0 copy-start.6
  1.3 0.0 copy-start
  1.3 1.6 %copy-done = bf16[1,1,64,128,128]{4,3,2,1,0:T(8,128)(2,1)S(1)} copy-done((bf16[1,1,64,128,128]{4,3,2,1,0:T(8,128)(2,1)S(1)}, bf16[1,1,64,128,128]{4,3,2,1,0:T(8,128)(2,1)}, u32[]{:S(2)}) %copy-start) | copy-done | bytes 2097176
  2.9 0.0 copy-start.1
  2.9 0.7 copy-done.1
  3.5 0.0 copy-start.2
  3.6 0.7 copy-done.2
  4.2 0.0 copy-start.3
  4.2 0.0 copy-start.4
  4.2 1.4 %block_matrix.1 = (bf16[1024,1024]{1,0:T(8,128)(2,1)S(1)}, s32[8,8,128]{2,1,0:T(8,128)S(1)}) custom-call(s32[64]{0:T(128)S(1)} %bitcast.12, s32[64]{0:T(128)S(1)} %bitcast.13, s32[1]{0:T(128)} %bitcast.9.refs_2_, bf16[64,128,128]{2,1,0:T(8,128)(2,1)S(1)} %bitcast.10), custom_call_target="tpu_custom_call" | custom-call | flops 1048576 | bytes 8388608 | tf_op jit(solution)/shard_map/block_matrix/pallas_call | solution.py:35
  5.6 0.0 copy-done.6
  5.7 0.0 copy-done.3
  5.7 0.1 copy-done.4
  5.7 0.0 copy-start.5
  5.7 1.0 copy-done.5
  6.7 94.1 %fused_layer.1 = (bf16[256,1024]{1,0:T(8,128)(2,1)S(1)}, bf16[256,768]{1,0:T(8,128)(2,1)S(1)}, bf16[2,2,2,96,1024]{4,3,2,1,0:T(8,128)(2,1)S(1)}, f32[8,128]{1,0:T(8,128)S(1)}) custom-call(bf16[1024,1024]{1,0:T(8,128)(2,1)S(1)} %get-tuple-element.10.refs_0_, bf16[256,768]{1,0:T(8,128)(2,1)S(1)} %copy-done.5, bf16[768,1024]{1,0:T(8,128)(2,1)S(1)} %copy-done.3, ...), custom_call_target="tpu_custom_call" | custom-call | flops 4429185024 | bytes 8388608 | tf_op jit(solution)/shard_map/fused_layer/pallas_call | solution.py:777
  100.8 2.2 %bitcast_convert_fusion = f32[768,1024]{1,0:T(8,128)} fusion(bf16[2,2,2,96,1024]{4,3,2,1,0:T(8,128)(2,1)S(1)} %get-tuple-element.14), kind=kLoop, calls=%fused_computation | loop fusion | flops 786432 | bytes 4718592 | tf_op jit(solution)/shard_map/convert_element_type | solution.py:825
  103.0 0.8 copy.16
  103.8 0.7 copy.17
  104.5 0.6 copy.18
Async XLA Ops:
  0.6 5.0 %copy-start.6 = (f32[1024]{0:T(1024)S(1)}, f32[1024]{0:T(1024)}, u32[]{:S(2)}) copy-start(f32[1024]{0:T(1024)} %param.14) | copy-start | bytes 12292
  1.3 1.6 %copy-start = (bf16[1,1,64,128,128]{4,3,2,1,0:T(8,128)(2,1)S(1)}, bf16[1,1,64,128,128]{4,3,2,1,0:T(8,128)(2,1)}, u32[]{:S(2)}) copy-start(bf16[1,1,64,128,128]{4,3,2,1,0:T(8,128)(2,1)} %param.9) | copy-start | bytes 6291460
  2.9 0.7 copy-start.1
  3.5 0.7 copy-start.2
  4.2 1.5 %copy-start.3 = (bf16[768,1024]{1,0:T(8,128)(2,1)S(1)}, bf16[768,1024]{1,0:T(8,128)(2,1)}, u32[]{:S(2)}) copy-start(bf16[768,1024]{1,0:T(8,128)(2,1)} %refs_2_.1) | copy-start | bytes 4718596
  4.2 1.5 %copy-start.4 = (bf16[256,1024]{1,0:T(8,128)(2,1)S(1)}, bf16[256,1024]{1,0:T(8,128)(2,1)}, u32[]{:S(2)}) copy-start(bf16[256,1024]{1,0:T(8,128)(2,1)} %refs_4_.1) | copy-start | bytes 1572868
  5.7 1.0 copy-start.5

commit v3 on v2

--- a/solution.py
+++ b/solution.py
@@ -529,7 +529,8 @@
         exchanges.remove(ex)
 
     back_ex = []
-    for f in range(chunks):
+
+    def launch(f):
         back = lax.dot_general(
             grad_b[...], weight[part(f), :], (((1,), (1,)), ((), ())), preferred_element_type=jnp.float32
         ).astype(jnp.bfloat16)
@@ -539,7 +540,7 @@
             exchanges.append(ex)
             ex.start(back)
             back_ex.append(ex)
-            continue
+            return
 
         def reply(k, carry, f=f, back=back):
             chosen = jnp.broadcast_to(asked[k, 0:1, :], (size, width))
@@ -554,6 +555,10 @@
         ex.start()
         back_ex.append(ex)
         back_in[f, at["d"]] = outbox[f, at["d"]]
+
+    lead = min(2, chunks)
+    for f in range(lead):
+        launch(f)
 
     agg_t[...] = agg[...].T
     w32[...] = jnp.dot(agg_t[...], grad_b[...], preferred_element_type=jnp.float32)
@@ -671,6 +676,8 @@
                 if ahead < chunks:
                     back_ex[ahead].relay()
         back_ex[f].arrive()
+        if f + lead < chunks:
+            launch(f + lead)
         given = back_in[f].reshape(D * size, width)
         for s in range(S):
             if flips:

time: 105 us -> 104 us (level)
  Pallas kernels: 95.5 us -> 93.8 us
    pallas_call x1, Pallas kernels: 94.1 us -> 92.4 us  [fused_layer(): pl.pallas_call(kernel, out_shape=(jax.ShapeDtypeStruct((rows, hid), bf),...]
where the time goes in v3:
time: 104 us; the launch traced here: 103 us
  Pallas kernels  93.8 us (90%)
  local copies, waits for them, and re-layouts  6.18 us (6%)
  other arithmetic  2.16 us (2%)
  between operations  1.34 us (1%)
    pallas_call x1, Pallas kernels, fused_layer(): pl.pallas_call(kernel, out_shape=(jax.ShapeDtypeStruct((rows, hid), bf),...  92.4 us
    unnamed x17, local copies, waits for them, and re-layouts  6.18 us
    convert_element_type x1, other arithmetic, per_device(): weight_grad = weight_part.reshape(feat, hid).astype(jnp.float32)  2.16 us

profile of v3, /device:TPU:0, one launch (start us, length us, event | category | flops | bytes accessed | tf_op | source)
XLA Modules:
  0.0 103.5 jit_solution(2911593715581633095)
XLA Ops:
  0.6 0.0 copy-start.6
  1.3 0.0 copy-start
  1.3 1.6 %copy-done = bf16[1,1,64,128,128]{4,3,2,1,0:T(8,128)(2,1)S(1)} copy-done((bf16[1,1,64,128,128]{4,3,2,1,0:T(8,128)(2,1)S(1)}, bf16[1,1,64,128,128]{4,3,2,1,0:T(8,128)(2,1)}, u32[]{:S(2)}) %copy-start) | copy-done | bytes 2097176
  2.9 0.0 copy-start.1
  2.9 0.7 copy-done.1
  3.5 0.0 copy-start.2
  3.6 0.7 copy-done.2
  4.2 0.0 copy-start.3
  4.2 0.0 copy-start.4
  4.2 1.3 %block_matrix.1 = (bf16[1024,1024]{1,0:T(8,128)(2,1)S(1)}, s32[8,8,128]{2,1,0:T(8,128)S(1)}) custom-call(s32[64]{0:T(128)S(1)} %bitcast.12, s32[64]{0:T(128)S(1)} %bitcast.13, s32[1]{0:T(128)} %bitcast.9.refs_2_, bf16[64,128,128]{2,1,0:T(8,128)(2,1)S(1)} %bitcast.10), custom_call_target="tpu_custom_call" | custom-call | flops 1048576 | bytes 8388608 | tf_op jit(solution)/shard_map/block_matrix/pallas_call | solution.py:35
  5.6 0.0 copy-done.6
  5.6 0.0 copy-done.3
  5.6 0.1 copy-done.4
  5.7 0.0 copy-start.5
  5.7 1.0 copy-done.5
  6.7 92.4 %fused_layer.1 = (bf16[256,1024]{1,0:T(8,128)(2,1)S(1)}, bf16[256,768]{1,0:T(8,128)(2,1)S(1)}, bf16[2,2,2,96,1024]{4,3,2,1,0:T(8,128)(2,1)S(1)}, f32[8,128]{1,0:T(8,128)S(1)}) custom-call(bf16[1024,1024]{1,0:T(8,128)(2,1)S(1)} %get-tuple-element.10.refs_0_, bf16[256,768]{1,0:T(8,128)(2,1)S(1)} %copy-done.5, bf16[768,1024]{1,0:T(8,128)(2,1)S(1)} %copy-done.3, ...), custom_call_target="tpu_custom_call" | custom-call | flops 4429185024 | bytes 8388608 | tf_op jit(solution)/shard_map/fused_layer/pallas_call | solution.py:784
  99.2 2.2 %bitcast_convert_fusion = f32[768,1024]{1,0:T(8,128)} fusion(bf16[2,2,2,96,1024]{4,3,2,1,0:T(8,128)(2,1)S(1)} %get-tuple-element.14), kind=kLoop, calls=%fused_computation | loop fusion | flops 786432 | bytes 4718592 | tf_op jit(solution)/shard_map/convert_element_type | solution.py:832
  101.3 0.8 copy.16
  102.1 0.7 copy.17
  102.9 0.6 copy.18
Async XLA Ops:
  0.6 4.9 %copy-start.6 = (f32[1024]{0:T(1024)S(1)}, f32[1024]{0:T(1024)}, u32[]{:S(2)}) copy-start(f32[1024]{0:T(1024)} %param.14) | copy-start | bytes 12292
  1.3 1.6 %copy-start = (bf16[1,1,64,128,128]{4,3,2,1,0:T(8,128)(2,1)S(1)}, bf16[1,1,64,128,128]{4,3,2,1,0:T(8,128)(2,1)}, u32[]{:S(2)}) copy-start(bf16[1,1,64,128,128]{4,3,2,1,0:T(8,128)(2,1)} %param.9) | copy-start | bytes 6291460
  2.9 0.7 copy-start.1
  3.5 0.7 copy-start.2
  4.2 1.4 %copy-start.3 = (bf16[768,1024]{1,0:T(8,128)(2,1)S(1)}, bf16[768,1024]{1,0:T(8,128)(2,1)}, u32[]{:S(2)}) copy-start(bf16[768,1024]{1,0:T(8,128)(2,1)} %refs_2_.1) | copy-start | bytes 4718596
  4.2 1.5 %copy-start.4 = (bf16[256,1024]{1,0:T(8,128)(2,1)S(1)}, bf16[256,1024]{1,0:T(8,128)(2,1)}, u32[]{:S(2)}) copy-start(bf16[256,1024]{1,0:T(8,128)(2,1)} %refs_4_.1) | copy-start | bytes 1572868
  5.7 1.0 copy-start.5
